TPU v7x, 32 devices: a whole 2x2x4 slice. The times are simulated.
32 devices in a mesh: row: 8 (over z, x), col: 4 (over y, core).
Axes of the slice: x: 2, y: 2, z: 4, core: 2. Of those that a mesh axis runs over, the one named last changes fastest.
Arguments:
- eigvecs: float32 [2048, 512], P('row', 'col'), may hold values from -6 to 6
- reflectors: float32 [8, 32, 128, 64], P(None, ('row', 'col')), may hold values from -2 to 2, as said below
- factors: float32 [8, 32, 64, 64], P(None, ('row', 'col')), may hold values from -3 to 3, as said below
- order: int32 [8], replicated, may hold values from 0 to 7, each once
- offsets: int32 [8], replicated, may hold values from 0 to 63
Outputs:
- rotated: float32 [2048, 512], P('row', 'col')
Inputs may be any that keep to these rules, and one draw needn't show every extreme that they name: `order`: a permutation of 0 .. 7. Every block map is orthogonal: with V the block of reflectors and T the block of factors, T is upper triangular and T^-1 + T^-T = V^T V. `factors`: upper triangular, paired with reflectors as promised there.
All inputs are finite; a program needn't handle non-finite values.
Results may differ from a plain program's by a relative error of at most 0.0003.
Values sent between devices are 32-bit elements; how exact they have to be, the bound alone decides.
A program may use at most 64 MiB of HBM per device.

v0:
```python
import jax
import jax.numpy as jnp
from jax import lax
from jax.sharding import PartitionSpec as P

highest = lax.Precision.HIGHEST


def passed_along(block, axis, distance):
    devices = range(lax.axis_size(axis))
    route = [(i - distance, i) for i in devices if i - distance in devices]
    return lax.ppermute(block, axis, route)


def entering(array, axis, combine, identity):
    size, position = (lax.axis_size(axis), lax.axis_index(axis))
    everything = jax.tree.map(lambda part: lax.all_gather(part, axis), array)
    start = jax.tree.map(
        lambda part, zero: jnp.broadcast_to(jnp.asarray(zero, part.dtype), part.shape),
        array,
        identity,
    )

    def hop(k, before):
        reached = k < position
        new = combine(before, jax.tree.map(lambda part: part[k], everything))
        return jax.tree.map(lambda a, b: jnp.where(reached, a, b), new, before)

    return lax.fori_loop(0, size, hop, start)


def reflect(segment, householder, triangle):
    inner = jnp.dot(householder.T, segment, precision=highest, preferred_element_type=jnp.float32)
    inner = jnp.dot(triangle, inner, precision=highest, preferred_element_type=jnp.float32)
    return segment - jnp.dot(
        householder, inner, precision=highest, preferred_element_type=jnp.float32
    )


def sweep_apply(extended, house_set, tri_set, offset):
    block_width = house_set.shape[-1]

    def advance(number, current):
        start = offset + number * block_width
        segment = lax.dynamic_slice_in_dim(current, start, 2 * block_width, 0)
        householder = lax.dynamic_index_in_dim(house_set, number, 0, keepdims=False)
        triangle = lax.dynamic_index_in_dim(tri_set, number, 0, keepdims=False)
        return lax.dynamic_update_slice_in_dim(
            current, reflect(segment, householder, triangle), start, 0
        )

    return lax.fori_loop(0, house_set.shape[0], advance, extended)


def compose(earlier, later):
    first_map = jnp.dot(later[0], earlier[0], precision=highest, preferred_element_type=jnp.float32)
    shifted = (
        jnp.dot(later[0], earlier[1], precision=highest, preferred_element_type=jnp.float32)
        + later[1]
    )
    return (first_map, shifted)


def local(eigvecs, reflectors, factors, order, offsets):
    height = eigvecs.shape[0]
    columns = eigvecs.shape[1]
    block_width = reflectors.shape[-1]
    span_rows = 2 * block_width
    leading = lax.axis_index("row") == 0
    identity = jnp.eye(span_rows, dtype=jnp.float32)
    probe = jnp.concatenate([identity, jnp.zeros((height, span_rows), jnp.float32)], 0)
    vectors = eigvecs
    for position in range(order.shape[0]):
        stored = order[position]
        offset = offsets[stored]
        own_house = lax.dynamic_index_in_dim(reflectors, stored, 0, keepdims=False)
        own_tri = lax.dynamic_index_in_dim(factors, stored, 0, keepdims=False)
        house_set, tri_set = (
            lax.all_gather(own_house, "col", axis=0, tiled=True),
            lax.all_gather(own_tri, "col", axis=0, tiled=True),
        )
        next_rows = passed_along(vectors[:span_rows], "row", -1)
        top_rows = jnp.where(leading, vectors[:span_rows], 0.0)
        extended = jnp.concatenate([top_rows, vectors[span_rows:], next_rows], 0)
        joined = sweep_apply(jnp.concatenate([extended, probe], 1), house_set, tri_set, offset)
        partial_value = joined[:, :columns]
        response = joined[:, columns:]
        transfer = jnp.where(leading, 0.0, response[height:])
        empty = jnp.zeros((span_rows, columns), jnp.float32)
        composed = entering((transfer, partial_value[height:]), "row", compose, (identity, empty))
        incoming = composed[1]
        vectors = partial_value[:height] + jnp.dot(
            response[:height], incoming, precision=highest, preferred_element_type=jnp.float32
        )
    return vectors


def solution(mesh):
    placed = (
        P("row", "col"),
        P(None, ("row", "col"), None, None),
        P(None, ("row", "col"), None, None),
        P(),
        P(),
    )
    return jax.shard_map(
        local, mesh=mesh, in_specs=placed, out_specs=P("row", "col"), check_vma=False
    )
```

profile of v0, /device:TPU:30, one launch (start us, length us, event | category | flops | bytes accessed | tf_op | source)
XLA Modules:
  0.0 717.8 jit_solution(1707958535803900348)
XLA Ops:
  33.1 9.5 %while.216 = (s32[]{:T(128)}, f32[384,256]{1,0:T(8,128)S(1)}, s32[]{:T(128)}, f32[4,128,64]{1,2,0:T(8,128)S(1)}, f32[4,64,64]{2,1,0:T(8,128)S(1)}, /*index=5*/s32[]{:T(128)}, s32[]{:T(128)}, s32[]{:T(128)}, s32[]{:T(128)}) while((s32[]{:T(128)}, f32[384,256]{1,0:T(8,128)S(1)}, s32[]{:T(128)}, f32[4,128,64]{1,2,0:T(8,128)S(1)}, ...), condition=%wide.region_1.2_spmd, body=%wide.region_0.1_spmd.sunk | while | flops 62947336 | bytes 1015983 | solution.py:52
  42.6 31.4 %all-gather.2 = f32[1024,128]{1,0:T(8,128)S(1)} all-gather(f32[128,128]{1,0:T(8,128)S(1)} %get-tuple-element.1884), channel_id=4, replica_groups=mesh['row'=8,'col'=4] {'row'}, dimensions={0}, use_global_device_ids=true | all-gather | bytes 589824 | tf_op jit(solution)/shard_map/all_gather | solution.py:17
  74.0 31.8 %all-gather.3 = f32[1024,128]{1,0:T(8,128)S(1)} all-gather(f32[128,128]{1,0:T(8,128)S(1)} %get-tuple-element.1883), channel_id=5, replica_groups=mesh['row'=8,'col'=4] {'row'}, dimensions={0}, use_global_device_ids=true | all-gather | bytes 589824 | tf_op jit(solution)/shard_map/all_gather | solution.py:17
  120.2 9.4 %while.217 = (s32[]{:T(128)}, f32[384,256]{1,0:T(8,128)S(1)}, s32[]{:T(128)}, f32[4,128,64]{1,2,0:T(8,128)S(1)}, f32[4,64,64]{2,1,0:T(8,128)S(1)}, /*index=5*/s32[]{:T(128)}, s32[]{:T(128)}, s32[]{:T(128)}, s32[]{:T(128)}) while((s32[]{:T(128)}, f32[384,256]{1,0:T(8,128)S(1)}, s32[]{:T(128)}, f32[4,128,64]{1,2,0:T(8,128)S(1)}, ...), condition=%wide.region_5.6_spmd, body=%wide.region_4.5_spmd.sunk | while | flops 62947336 | bytes 1015983 | solution.py:52
  129.6 31.5 %all-gather.6 = f32[1024,128]{1,0:T(8,128)S(1)} all-gather(f32[128,128]{1,0:T(8,128)S(1)} %get-tuple-element.1882), channel_id=8, replica_groups=mesh['row'=8,'col'=4] {'row'}, dimensions={0}, use_global_device_ids=true | all-gather | bytes 589824 | tf_op jit(solution)/shard_map/all_gather | solution.py:17
  161.1 31.7 %all-gather.7 = f32[1024,128]{1,0:T(8,128)S(1)} all-gather(f32[128,128]{1,0:T(8,128)S(1)} %get-tuple-element.1881), channel_id=9, replica_groups=mesh['row'=8,'col'=4] {'row'}, dimensions={0}, use_global_device_ids=true | all-gather | bytes 589824 | tf_op jit(solution)/shard_map/all_gather | solution.py:17
  207.3 9.2 %while.218 = (s32[]{:T(128)}, f32[384,256]{1,0:T(8,128)S(1)}, s32[]{:T(128)}, f32[4,128,64]{1,2,0:T(8,128)S(1)}, f32[4,64,64]{2,1,0:T(8,128)S(1)}, /*index=5*/s32[]{:T(128)}, s32[]{:T(128)}, s32[]{:T(128)}, s32[]{:T(128)}) while((s32[]{:T(128)}, f32[384,256]{1,0:T(8,128)S(1)}, s32[]{:T(128)}, f32[4,128,64]{1,2,0:T(8,128)S(1)}, ...), condition=%wide.region_9.10_spmd, body=%wide.region_8.9_spmd.sunk | while | flops 62947336 | bytes 1015983 | solution.py:52
  216.5 31.7 %all-gather.10 = f32[1024,128]{1,0:T(8,128)S(1)} all-gather(f32[128,128]{1,0:T(8,128)S(1)} %get-tuple-element.1880), channel_id=12, replica_groups=mesh['row'=8,'col'=4] {'row'}, dimensions={0}, use_global_device_ids=true | all-gather | bytes 589824 | tf_op jit(solution)/shard_map/all_gather | solution.py:17
  248.2 31.7 %all-gather.11 = f32[1024,128]{1,0:T(8,128)S(1)} all-gather(f32[128,128]{1,0:T(8,128)S(1)} %get-tuple-element.1879), channel_id=13, replica_groups=mesh['row'=8,'col'=4] {'row'}, dimensions={0}, use_global_device_ids=true | all-gather | bytes 589824 | tf_op jit(solution)/shard_map/all_gather | solution.py:17
  294.3 9.5 %while.219 = (s32[]{:T(128)}, f32[384,256]{1,0:T(8,128)S(1)}, s32[]{:T(128)}, f32[4,128,64]{1,2,0:T(8,128)S(1)}, f32[4,64,64]{2,1,0:T(8,128)S(1)}, /*index=5*/s32[]{:T(128)}, s32[]{:T(128)}, s32[]{:T(128)}, s32[]{:T(128)}) while((s32[]{:T(128)}, f32[384,256]{1,0:T(8,128)S(1)}, s32[]{:T(128)}, f32[4,128,64]{1,2,0:T(8,128)S(1)}, ...), condition=%wide.region_13.14_spmd, body=%wide.region_12.13_spmd.sunk | while | flops 62947336 | bytes 1015983 | solution.py:52
  303.8 31.4 %all-gather.14 = f32[1024,128]{1,0:T(8,128)S(1)} all-gather(f32[128,128]{1,0:T(8,128)S(1)} %get-tuple-element.1878), channel_id=16, replica_groups=mesh['row'=8,'col'=4] {'row'}, dimensions={0}, use_global_device_ids=true | all-gather | bytes 589824 | tf_op jit(solution)/shard_map/all_gather | solution.py:17
  335.2 31.6 %all-gather.15 = f32[1024,128]{1,0:T(8,128)S(1)} all-gather(f32[128,128]{1,0:T(8,128)S(1)} %get-tuple-element.1877), channel_id=17, replica_groups=mesh['row'=8,'col'=4] {'row'}, dimensions={0}, use_global_device_ids=true | all-gather | bytes 589824 | tf_op jit(solution)/shard_map/all_gather | solution.py:17
  381.3 9.6 %while.220 = (s32[]{:T(128)}, f32[384,256]{1,0:T(8,128)S(1)}, s32[]{:T(128)}, f32[4,128,64]{1,2,0:T(8,128)S(1)}, f32[4,64,64]{2,1,0:T(8,128)S(1)}, /*index=5*/s32[]{:T(128)}, s32[]{:T(128)}, s32[]{:T(128)}, s32[]{:T(128)}) while((s32[]{:T(128)}, f32[384,256]{1,0:T(8,128)S(1)}, s32[]{:T(128)}, f32[4,128,64]{1,2,0:T(8,128)S(1)}, ...), condition=%wide.region_17.18_spmd, body=%wide.region_16.17_spmd.sunk | while | flops 62947336 | bytes 1015983 | solution.py:52
  390.9 31.4 %all-gather.18 = f32[1024,128]{1,0:T(8,128)S(1)} all-gather(f32[128,128]{1,0:T(8,128)S(1)} %get-tuple-element.1876), channel_id=20, replica_groups=mesh['row'=8,'col'=4] {'row'}, dimensions={0}, use_global_device_ids=true | all-gather | bytes 589824 | tf_op jit(solution)/shard_map/all_gather | solution.py:17
  422.4 31.6 %all-gather.19 = f32[1024,128]{1,0:T(8,128)S(1)} all-gather(f32[128,128]{1,0:T(8,128)S(1)} %get-tuple-element.1875), channel_id=21, replica_groups=mesh['row'=8,'col'=4] {'row'}, dimensions={0}, use_global_device_ids=true | all-gather | bytes 589824 | tf_op jit(solution)/shard_map/all_gather | solution.py:17
  468.5 9.3 %while.221 = (s32[]{:T(128)}, f32[384,256]{1,0:T(8,128)S(1)}, s32[]{:T(128)}, f32[4,128,64]{1,2,0:T(8,128)S(1)}, f32[4,64,64]{2,1,0:T(8,128)S(1)}, /*index=5*/s32[]{:T(128)}, s32[]{:T(128)}, s32[]{:T(128)}, s32[]{:T(128)}) while((s32[]{:T(128)}, f32[384,256]{1,0:T(8,128)S(1)}, s32[]{:T(128)}, f32[4,128,64]{1,2,0:T(8,128)S(1)}, ...), condition=%wide.region_21.22_spmd, body=%wide.region_20.21_spmd.sunk | while | flops 62947336 | bytes 1015983 | solution.py:52
  477.8 31.6 %all-gather.22 = f32[1024,128]{1,0:T(8,128)S(1)} all-gather(f32[128,128]{1,0:T(8,128)S(1)} %get-tuple-element.1874), channel_id=24, replica_groups=mesh['row'=8,'col'=4] {'row'}, dimensions={0}, use_global_device_ids=true | all-gather | bytes 589824 | tf_op jit(solution)/shard_map/all_gather | solution.py:17
  509.4 31.5 %all-gather.23 = f32[1024,128]{1,0:T(8,128)S(1)} all-gather(f32[128,128]{1,0:T(8,128)S(1)} %get-tuple-element.1873), channel_id=25, replica_groups=mesh['row'=8,'col'=4] {'row'}, dimensions={0}, use_global_device_ids=true | all-gather | bytes 589824 | tf_op jit(solution)/shard_map/all_gather | solution.py:17
  555.6 9.1 %while.222 = (s32[]{:T(128)}, f32[384,256]{1,0:T(8,128)S(1)}, s32[]{:T(128)}, f32[4,128,64]{1,2,0:T(8,128)S(1)}, f32[4,64,64]{2,1,0:T(8,128)S(1)}, /*index=5*/s32[]{:T(128)}, s32[]{:T(128)}, s32[]{:T(128)}, s32[]{:T(128)}) while((s32[]{:T(128)}, f32[384,256]{1,0:T(8,128)S(1)}, s32[]{:T(128)}, f32[4,128,64]{1,2,0:T(8,128)S(1)}, ...), condition=%wide.region_25.26_spmd, body=%wide.region_24.25_spmd.sunk | while | flops 62947336 | bytes 1015983 | solution.py:52
  564.7 31.5 %all-gather.26 = f32[1024,128]{1,0:T(8,128)S(1)} all-gather(f32[128,128]{1,0:T(8,128)S(1)} %get-tuple-element.1872), channel_id=28, replica_groups=mesh['row'=8,'col'=4] {'row'}, dimensions={0}, use_global_device_ids=true | all-gather | bytes 589824 | tf_op jit(solution)/shard_map/all_gather | solution.py:17
  596.2 31.6 %all-gather.27 = f32[1024,128]{1,0:T(8,128)S(1)} all-gather(f32[128,128]{1,0:T(8,128)S(1)} %get-tuple-element.1871), channel_id=29, replica_groups=mesh['row'=8,'col'=4] {'row'}, dimensions={0}, use_global_device_ids=true | all-gather | bytes 589824 | tf_op jit(solution)/shard_map/all_gather | solution.py:17
  642.2 9.5 %while.223 = (s32[]{:T(128)}, f32[384,256]{1,0:T(8,128)S(1)}, s32[]{:T(128)}, f32[4,128,64]{1,2,0:T(8,128)S(1)}, f32[4,64,64]{2,1,0:T(8,128)S(1)}, /*index=5*/s32[]{:T(128)}, s32[]{:T(128)}, s32[]{:T(128)}, s32[]{:T(128)}) while((s32[]{:T(128)}, f32[384,256]{1,0:T(8,128)S(1)}, s32[]{:T(128)}, f32[4,128,64]{1,2,0:T(8,128)S(1)}, ...), condition=%wide.region_29.30_spmd, body=%wide.region_28.29_spmd.sunk | while | flops 62947336 | bytes 1015983 | solution.py:52
  651.7 31.5 %all-gather.30 = f32[1024,128]{1,0:T(8,128)S(1)} all-gather(f32[128,128]{1,0:T(8,128)S(1)} %get-tuple-element.1870), channel_id=32, replica_groups=mesh['row'=8,'col'=4] {'row'}, dimensions={0}, use_global_device_ids=true | all-gather | bytes 589824 | tf_op jit(solution)/shard_map/all_gather | solution.py:17
  683.2 31.7 %all-gather.31 = f32[1024,128]{1,0:T(8,128)S(1)} all-gather(f32[128,128]{1,0:T(8,128)S(1)} %get-tuple-element.1869), channel_id=33, replica_groups=mesh['row'=8,'col'=4] {'row'}, dimensions={0}, use_global_device_ids=true | all-gather | bytes 589824 | tf_op jit(solution)/shard_map/all_gather | solution.py:17
  (350 shorter events, 187.5 us)
Async XLA Ops:
  0.0 19.9 %copy-start = (f32[8,1,128,64]{2,3,1,0:T(8,128)S(1)}, f32[8,1,128,64]{2,3,1,0:T(8,128)}, u32[]{:S(2)}) copy-start(f32[8,1,128,64]{2,3,1,0:T(8,128)} %param.38) | copy-start | bytes 786436
  0.9 2.5 copy-start.3
  0.9 32.1 %collective-permute-start = (f32[128,128]{1,0:T(8,128)S(1)}, f32[128,128]{1,0:T(8,128)S(1)}, u32[]{:S(2)}, u32[]{:S(2)}) collective-permute-start(f32[128,128]{1,0:T(8,128)S(1)} %get-tuple-element.1924), channel_id=1, source_target_pairs={{4,0},{8,4},{12,8},{16,12},{20,16},{24,20},{28,24},{5,1},{9,5},{13... | collective-permute-start | bytes 196616 | tf_op jit(solution)/shard_map/ppermute | solution.py:12
  19.9 1.0 copy-start.1
  20.9 0.7 copy-start.2
  108.1 12.1 %collective-permute-start.1 = (f32[128,128]{1,0:T(8,128)S(1)}, f32[128,128]{1,0:T(8,128)S(1)}, u32[]{:S(2)}, u32[]{:S(2)}) collective-permute-start(f32[128,128]{1,0:T(8,128)S(1)} %get-tuple-element.1921), channel_id=1, source_target_pairs={{4,0},{8,4},{12,8},{16,12},{20,16},{24,20},{28,24},{5,1},{9,5},{13... | collective-permute-start | bytes 196616 | tf_op jit(solution)/shard_map/ppermute | solution.py:12
  195.1 12.1 %collective-permute-start.2 = (f32[128,128]{1,0:T(8,128)S(1)}, f32[128,128]{1,0:T(8,128)S(1)}, u32[]{:S(2)}, u32[]{:S(2)}) collective-permute-start(f32[128,128]{1,0:T(8,128)S(1)} %get-tuple-element.1918), channel_id=1, source_target_pairs={{4,0},{8,4},{12,8},{16,12},{20,16},{24,20},{28,24},{5,1},{9,5},{13... | collective-permute-start | bytes 196616 | tf_op jit(solution)/shard_map/ppermute | solution.py:12
  282.1 12.1 %collective-permute-start.3 = (f32[128,128]{1,0:T(8,128)S(1)}, f32[128,128]{1,0:T(8,128)S(1)}, u32[]{:S(2)}, u32[]{:S(2)}) collective-permute-start(f32[128,128]{1,0:T(8,128)S(1)} %get-tuple-element.1915), channel_id=1, source_target_pairs={{4,0},{8,4},{12,8},{16,12},{20,16},{24,20},{28,24},{5,1},{9,5},{13... | collective-permute-start | bytes 196616 | tf_op jit(solution)/shard_map/ppermute | solution.py:12
  369.1 12.1 %collective-permute-start.4 = (f32[128,128]{1,0:T(8,128)S(1)}, f32[128,128]{1,0:T(8,128)S(1)}, u32[]{:S(2)}, u32[]{:S(2)}) collective-permute-start(f32[128,128]{1,0:T(8,128)S(1)} %get-tuple-element.1912), channel_id=1, source_target_pairs={{4,0},{8,4},{12,8},{16,12},{20,16},{24,20},{28,24},{5,1},{9,5},{13... | collective-permute-start | bytes 196616 | tf_op jit(solution)/shard_map/ppermute | solution.py:12
  456.3 12.1 %collective-permute-start.5 = (f32[128,128]{1,0:T(8,128)S(1)}, f32[128,128]{1,0:T(8,128)S(1)}, u32[]{:S(2)}, u32[]{:S(2)}) collective-permute-start(f32[128,128]{1,0:T(8,128)S(1)} %get-tuple-element.1909), channel_id=1, source_target_pairs={{4,0},{8,4},{12,8},{16,12},{20,16},{24,20},{28,24},{5,1},{9,5},{13... | collective-permute-start | bytes 196616 | tf_op jit(solution)/shard_map/ppermute | solution.py:12
  543.2 12.3 %collective-permute-start.6 = (f32[128,128]{1,0:T(8,128)S(1)}, f32[128,128]{1,0:T(8,128)S(1)}, u32[]{:S(2)}, u32[]{:S(2)}) collective-permute-start(f32[128,128]{1,0:T(8,128)S(1)} %get-tuple-element.1906), channel_id=1, source_target_pairs={{4,0},{8,4},{12,8},{16,12},{20,16},{24,20},{28,24},{5,1},{9,5},{13... | collective-permute-start | bytes 196616 | tf_op jit(solution)/shard_map/ppermute | solution.py:12
  630.0 12.1 %collective-permute-start.7 = (f32[128,128]{1,0:T(8,128)S(1)}, f32[128,128]{1,0:T(8,128)S(1)}, u32[]{:S(2)}, u32[]{:S(2)}) collective-permute-start(f32[128,128]{1,0:T(8,128)S(1)} %get-tuple-element.1903), channel_id=1, source_target_pairs={{4,0},{8,4},{12,8},{16,12},{20,16},{24,20},{28,24},{5,1},{9,5},{13... | collective-permute-start | bytes 196616 | tf_op jit(solution)/shard_map/ppermute | solution.py:12
where the time goes:
time: 721 us; the launch traced here: 718 us
  blocking collectives  592 us (82%)
  matrix products  39.6 us (5%)
  local copies, waits for them, and re-layouts  32.3 us (4%)
  loops' own time  24.8 us (3%)
  between operations  16.3 us (2%)
  starting transfers between devices  11.5 us (2%)
    all_gather x16, blocking collectives, entering(): everything = jax.tree.map(lambda part: lax.all_gather(part, axis), array)  505 us
    all_gather x8, blocking collectives, local(): lax.all_gather(own_tri, 'col', axis=0, tiled=True)  43.5 us
    all_gather x8, blocking collectives, local(): lax.all_gather(own_house, 'col', axis=0, tiled=True)  43.2 us
    dynamic_update_slice x32, local copies, waits for them, and re-layouts, advance(): lax.dynamic_update_slice_in_dim(current, reflect(segment, householder, tr...  28.9 us
    another operation x8, loops' own time, sweep_apply(): return lax.fori_loop(0, house_set.shape[0], advance, extended)  22.6 us
  transfers between devices with their start and end apart: 8, of which 0 were waited for; matrix products, arithmetic and copies ran while one was open for 0% of the time, Pallas kernels for 0%

commit v1 on v0

--- a/solution.py
+++ b/solution.py
@@ -1,9 +1,112 @@
+import functools
+
 import jax
 import jax.numpy as jnp
 from jax import lax
+from jax.experimental import pallas as pl
+from jax.experimental.pallas import tpu as pltpu
 from jax.sharding import PartitionSpec as P
 
 highest = lax.Precision.HIGHEST
+LAG = 3
+
+
+def split(x):
+    hi = x.astype(jnp.bfloat16)
+    lo = (x - hi.astype(jnp.float32)).astype(jnp.bfloat16)
+    return hi, lo
+
+
+def product(a, b):
+    a_hi, a_lo = split(a)
+    b_hi, b_lo = split(b)
+    dot = functools.partial(jnp.dot, preferred_element_type=jnp.float32)
+    return dot(a_hi, b_hi) + (dot(a_hi, b_lo) + dot(a_lo, b_hi))
+
+
+def wave(sweeps, blocks, width, order_ref, off_ref, x_ref, *refs):
+    maps, (out_ref, frames, carry) = refs[:sweeps], refs[sweeps:]
+    step = pl.program_id(0)
+    height = x_ref.shape[0]
+    pad = 2 * width
+
+    @pl.when(step == 0)
+    def _():
+        frames[0, pl.ds(pad, height), :] = x_ref[...]
+
+    loaded = []
+    for p in range(sweeps):
+        k = step - 2 - LAG * p
+        here = off_ref[order_ref[p]]
+        before = off_ref[order_ref[p - 1]] if p else 0
+        at = jnp.clip(k, -2, blocks - 1)
+        rows = frames[p, pl.ds((at + 1) * width + here - before + pad, width), :]
+        index = (at + 1) * width + here + lax.broadcasted_iota(jnp.int32, rows.shape, 0)
+        rows = jnp.where(index < height, rows, 0.0)
+        loaded.append(jnp.concatenate([carry[p], rows], 0))
+    results = []
+    for p in range(sweeps):
+        k = step - 2 - LAG * p
+        moved = product(maps[p][0, 0], loaded[p])
+        results.append(jnp.where(k >= 0, moved, loaded[p]))
+    for p in range(sweeps):
+        k = step - 2 - LAG * p
+        spot = jnp.clip(k, -2, blocks) + 2
+        frames[p + 1, pl.ds(pl.multiple_of(spot * width, width), width), :] = results[p][:width]
+        carry[p] = results[p][width:]
+
+    @pl.when(step == pl.num_programs(0) - 1)
+    def _():
+        last = off_ref[order_ref[sweeps - 1]]
+
+        def put(n, _):
+            at = pl.multiple_of(n * width, width)
+            out_ref[pl.ds(at, width), :] = frames[sweeps, pl.ds(at + pad - last, width), :]
+            return 0
+
+        lax.fori_loop(0, height // width, put, 0)
+
+
+def sweep_all(vectors, maps, order, offsets):
+    blocks, sweeps, span, _ = maps.shape
+    width = span // 2
+    height, columns = vectors.shape
+    steps = blocks + 2 + LAG * (sweeps - 1)
+
+    def map_spec(p):
+        return pl.BlockSpec(
+            (1, 1, span, span),
+            lambda w, *_: (jnp.clip(w - 2 - LAG * p, 0, blocks - 1), p, 0, 0),
+        )
+
+    return pl.pallas_call(
+        functools.partial(wave, sweeps, blocks, width),
+        out_shape=jax.ShapeDtypeStruct((height, columns), jnp.float32),
+        grid_spec=pltpu.PrefetchScalarGridSpec(
+            num_scalar_prefetch=2,
+            grid=(steps,),
+            in_specs=[pl.BlockSpec((height, columns), lambda w, *_: (0, 0))]
+            + [map_spec(p) for p in range(sweeps)],
+            out_specs=pl.BlockSpec((height, columns), lambda w, *_: (0, 0)),
+            scratch_shapes=[
+                pltpu.VMEM((sweeps + 1, (blocks + 5) * width, columns), jnp.float32),
+                pltpu.VMEM((sweeps, width, columns), jnp.float32),
+            ],
+        ),
+        compiler_params=pltpu.CompilerParams(dimension_semantics=("arbitrary",)),
+    )(order, offsets, vectors, *([maps] * sweeps))
+
+
+def wavefront(eigvecs, reflectors, factors, order, offsets):
+    house = reflectors[order, 0]
+    tri = factors[order, 0]
+    scaled = jnp.einsum("sab,sbc->sac", house, tri, precision=highest)
+    inner = jnp.einsum("sab,scb->sac", scaled, house, precision=highest)
+    own = jnp.eye(inner.shape[-1], dtype=jnp.float32) - inner
+    maps = lax.all_gather(own, ("row", "col"), axis=0, tiled=False)
+    strip = lax.all_to_all(eigvecs, "row", split_axis=1, concat_axis=0, tiled=True)
+    moved = sweep_all(strip, maps, order, offsets)
+    return lax.all_to_all(moved, "row", split_axis=0, concat_axis=1, tiled=True)
 
 
 def passed_along(block, axis, distance):
@@ -103,6 +206,14 @@
         P(),
         P(),
     )
+
+    def run(eigvecs, reflectors, factors, order, offsets):
+        sweeps, count, span, _ = reflectors.shape
+        gathered = 4 * sweeps * count * mesh.size * span * span
+        fits = gathered <= 24 * 2**20 and eigvecs.shape[1] % mesh.shape["row"] == 0 and count == 1
+        body = wavefront if fits else local
+        return body(eigvecs, reflectors, factors, order, offsets)
+
     return jax.shard_map(
-        local, mesh=mesh, in_specs=placed, out_specs=P("row", "col"), check_vma=False
-    )
+        run, mesh=mesh, in_specs=placed, out_specs=P("row", "col"), check_vma=False
+    )

time: 721 us -> 192 us (0.27)
  the two profiles are of different devices: /device:TPU:30 before, /device:TPU:0 now
where the time goes in v1:
time: 192 us; the launch traced here: 190 us
  waiting for transfers between devices  100 us (52%)
  Pallas kernels  40.7 us (21%)
  blocking collectives  25.2 us (13%)
  between operations  13.4 us (7%)
  local copies, waits for them, and re-layouts  6.91 us (4%)
  matrix products  2.41 us (1%)
    all_gather x1, waiting for transfers between devices, wavefront(): maps = lax.all_gather(own, ('row', 'col'), axis=0, tiled=False)  100 us
    pallas_call x1, Pallas kernels, sweep_all(): pl.pallas_call(functools.partial(wave, sweeps, blocks, width), out_shape=...  40.7 us
    all_to_all x1, blocking collectives, wavefront(): lax.all_to_all(eigvecs, 'row', split_axis=1, concat_axis=0, tiled=True)  14.5 us
    all_to_all x1, blocking collectives, wavefront(): return lax.all_to_all(moved, 'row', split_axis=0, concat_axis=1, tiled=True)  10.7 us
  transfers between devices with their start and end apart: 1, of which 1 were waited for; matrix products, arithmetic and copies ran while one was open for 1% of the time, Pallas kernels for 0%

profile of v1, /device:TPU:0, one launch (start us, length us, event | category | flops | bytes accessed | tf_op | source)
XLA Modules:
  0.0 189.8 jit_solution(4681225753083568197)
XLA Ops:
  6.5 0.0 copy-start
  6.5 0.0 all-gather.3.cloned.1.call-start
  6.6 0.7 fusion.2
  7.3 0.2 copy-done
  7.5 0.6 gather_fusion
  8.1 1.5 gather_fusion.1
  9.6 0.6 fusion.3
  10.2 1.8 convolution_subtract_fusion
  12.0 0.0 all-gather.3.cloned.1.call-update
  12.0 1.0 copy.12
  13.0 14.5 %all_to_all.38 = f32[256,8,16]{0,2,1:T(8,128)S(1)} all-to-all(f32[256,8,16]{0,2,1:T(8,128)S(1)} %bitcast.24), channel_id=1, replica_groups=mesh['row'=8,'col'=4] {'row'}, dimensions={1} | all-to-all | bytes 262144 | tf_op jit(solution)/shard_map/all_to_all | solution.py:107
  27.6 1.3 copy.13
  28.9 100.4 %all-gather.3.cloned.1.call-done = f32[256,128,128]{2,1,0:T(8,128)} async-done(((f32[8,128,128]{2,1,0:T(8,128)}), f32[256,128,128]{2,1,0:T(8,128)}) %all-gather.3.cloned.1.call-update) | async-done | bytes 16777232 | tf_op jit(solution)/shard_map/all_gather | solution.py:106
  129.3 40.7 %shard_map.55 = f32[2048,16]{1,0:T(8,128)} custom-call(s32[8]{0:T(128)} %order_ref.1, s32[8]{0:T(128)} %off_ref.1, f32[2048,16]{1,0:T(8,128)} %bitcast.20, f32[32,8,128,128]{3,2,1,0:T(8,128)} %bitcast.12, f32[32,8,128,128]{3,2,1,0:T(8,128)} %bitcast.13, f32[32,8,128,128]{3,2,1,0:T(8,128)} %bitcast.14, f32[32,8,128,128]{3,2,1,0:T(8,128)} %bitcast.15, ...), custom_call_target="tpu_custom_call" | custom-call | tf_op jit(solution)/shard_map/pallas_call | solution.py:82
  170.0 1.5 copy.15
  171.5 10.7 %all_to_all.39 = f32[8,256,16]{1,2,0:T(8,128)S(1)} all-to-all(f32[8,256,16]{1,2,0:T(8,128)S(1)} %copy.15), channel_id=1, replica_groups=mesh['row'=8,'col'=4] {'row'}, dimensions={0} | all-to-all | bytes 262144 | tf_op jit(solution)/shard_map/all_to_all | solution.py:109
  182.2 0.8 copy.16
  (1 shorter events, 0.0 us)
Async XLA Ops:
  6.5 1.0 copy-start
  6.5 122.7 %all-gather.3.cloned.1.call-start = ((), (), s32[]{:S(2)}) async-start(), calls=%async_computation.2 | async-start | bytes 17301504 | tf_op jit(solution)/shard_map/all_gather | solution.py:106
Sparse Core Ops, SparseCore 0:
  12.2 117.0 all-gather.2

commit v2 on v0

v2 whole, which is shorter than its diff:
```python
import functools

import jax
import jax.numpy as jnp
from jax import lax
from jax.experimental import pallas as pl
from jax.experimental.pallas import tpu as pltpu
from jax.sharding import PartitionSpec as P

MESH = pl.DeviceIdType.MESH
highest = lax.Precision.HIGHEST


def split(x):
    hi = x.astype(jnp.bfloat16)
    lo = (x - hi.astype(jnp.float32)).astype(jnp.bfloat16)
    return hi, lo


def product(a, b):
    a_hi, a_lo = split(a)
    b_hi, b_lo = split(b)
    dot = functools.partial(jnp.dot, preferred_element_type=jnp.float32)
    return dot(a_hi, b_hi) + (dot(a_hi, b_lo) + dot(a_lo, b_hi))


def kernel(
    rows_n, cols_n, order_ref, off_ref, x_ref, house_ref, tri_ref, out_ref,
    maps, frames, up_in, down_in, down_out, last_in,
    map_send, map_recv, up_send, up_recv, down_send, down_recv, last_send, last_recv,
):
    row, col = lax.axis_index("row"), lax.axis_index("col")
    sweeps, span = maps.shape[1], maps.shape[2]
    width = span // 2
    height, columns = x_ref.shape
    per = height // width
    pad = span
    first, final = row == 0, row == rows_n - 1

    def peer(shift):
        return lax.rem(col + shift, cols_n)

    def map_copy(p, shift):
        return pltpu.make_async_remote_copy(
            src_ref=maps.at[col, p], dst_ref=maps.at[col, p],
            send_sem=map_send.at[shift - 1, p], recv_sem=map_recv.at[col, p],
            device_id=(row, peer(shift)), device_id_type=MESH,
        )

    def map_arrival(p, j):
        return pltpu.make_async_remote_copy(
            src_ref=maps.at[j, p], dst_ref=maps.at[j, p],
            send_sem=map_send.at[0, p], recv_sem=map_recv.at[j, p],
            device_id=(row, j), device_id_type=MESH,
        )

    def up_copy(q, part, src):
        return pltpu.make_async_remote_copy(
            src_ref=src, dst_ref=up_in.at[q, part],
            send_sem=up_send.at[q, part], recv_sem=up_recv.at[q, part],
            device_id=(row - 1, col), device_id_type=MESH,
        )

    def down_copy(q):
        return pltpu.make_async_remote_copy(
            src_ref=down_out.at[q], dst_ref=down_in.at[q],
            send_sem=down_send.at[q], recv_sem=down_recv.at[q],
            device_id=(row + 1, col), device_id_type=MESH,
        )

    def last_copy():
        return pltpu.make_async_remote_copy(
            src_ref=frames.at[sweeps, pl.ds(pad + height - width, width)], dst_ref=last_in,
            send_sem=last_send, recv_sem=last_recv,
            device_id=(row + 1, col), device_id_type=MESH,
        )

    def frame(q, part):
        return frames.at[q, pl.ds(pad + part * width, width)]

    barrier = pltpu.get_barrier_semaphore()
    for shift in range(1, cols_n):
        pl.semaphore_signal(barrier, inc=1, device_id=(row, peer(shift)), device_id_type=MESH)

    @pl.when(row > 0)
    def _():
        pl.semaphore_signal(barrier, inc=1, device_id=(row - 1, col), device_id_type=MESH)

    @pl.when(row < rows_n - 1)
    def _():
        pl.semaphore_signal(barrier, inc=1, device_id=(row + 1, col), device_id_type=MESH)

    def dense(p):
        house = house_ref[order_ref[p], 0]
        tri = tri_ref[order_ref[p], 0]
        scaled = jnp.dot(house, tri, precision=highest, preferred_element_type=jnp.float32)
        inner = lax.dot_general(
            scaled, house, (((1,), (1,)), ((), ())), precision=highest,
            preferred_element_type=jnp.float32,
        )
        eye = lax.broadcasted_iota(jnp.int32, inner.shape, 0) == lax.broadcasted_iota(
            jnp.int32, inner.shape, 1
        )
        maps[col, p] = jnp.where(eye, 1.0, 0.0) - inner

    dense(0)
    frames[0, pl.ds(pad, height), :] = x_ref[...]
    greeted = cols_n - 1 + jnp.minimum(row, 1) + jnp.minimum(rows_n - 1 - row, 1)
    pl.semaphore_wait(barrier, greeted)

    for shift in range(1, cols_n):
        map_copy(0, shift).start()

    @pl.when(row > 0)
    def _():
        for part in range(2):
            up_copy(0, part, x_ref.at[pl.ds(part * width, width)]).start()

    def spread(p, _):
        dense(p)
        for shift in range(1, cols_n):
            map_copy(p, shift).start()
        return 0

    lax.fori_loop(1, sweeps, spread, 0)

    def sweep(q, _):
        here = off_ref[order_ref[q]]
        before = jnp.where(q == 0, 0, off_ref[order_ref[jnp.maximum(q - 1, 0)]])
        move = here - before
        for j in range(cols_n):

            @pl.when(col != j)
            def _(j=j):
                map_arrival(q, j).wait_recv()

        def fresh(j):
            rows = frames[q, pl.ds(pad + (j + 1) * width + move, width), :]
            index = row * height + (j + 1) * width + here
            index = index + lax.broadcasted_iota(jnp.int32, rows.shape, 0)
            return jnp.where(index < rows_n * height, rows, 0.0)

        blank = jnp.zeros((width, columns), jnp.float32)

        def early(j):
            return product(maps[j, q], jnp.concatenate([blank, fresh(j)], 0))

        def late(j, ready, carried):
            return ready + product(maps[j, q], jnp.concatenate([carried, blank], 0))

        def arrive(part):
            @pl.when(row < rows_n - 1)
            def _():
                up_copy(q, part, up_in.at[q, part]).wait_recv()

            frames[q, pl.ds(pad + height + part * width, width), :] = up_in[q, part]

        ready = [early(j) for j in range(per - 2)]
        top = frames[q, pl.ds(pad - width + move, width), :]
        frames[q + 1, pl.ds(pad - width, width), :] = top
        own = frames[q, pl.ds(pad + move, width), :]

        @pl.when(row > 0)
        def _():
            down_copy(q).wait_recv()

        carried = jnp.where(first, own, down_in[q])
        for j in range(per):
            if j >= per - 2:
                arrive(j - (per - 2))
                ready.append(early(j))
            both = late(j, ready[j], carried)
            frames[q + 1, pl.ds(pad + j * width, width), :] = both[:width]
            carried = both[width:]
            if j < 2:

                @pl.when((row > 0) & (q < sweeps - 1))
                def _(j=j):
                    up_copy(q + 1, j, frame(q + 1, j)).start()

        down_out[q] = carried

        @pl.when(row < rows_n - 1)
        def _():
            down_copy(q).start()

        return 0

    lax.fori_loop(0, sweeps, sweep, 0)

    @pl.when(row < rows_n - 1)
    def _():
        last_copy().start()

    @pl.when(row > 0)
    def _():
        last_copy().wait_recv()

    edge = frames[sweeps, pl.ds(pad - width, width), :]
    frames[sweeps, pl.ds(pad - width, width), :] = jnp.where(first, edge, last_in[...])
    shift_back = off_ref[order_ref[sweeps - 1]]
    out_ref[...] = frames[sweeps, pl.ds(pad - shift_back, height), :]

    def drain(p, _):
        for shift in range(1, cols_n):
            map_copy(p, shift).wait_send()

        @pl.when(row > 0)
        def _():
            for part in range(2):
                up_copy(p, part, up_in.at[p, part]).wait_send()

        @pl.when(row < rows_n - 1)
        def _():
            down_copy(p).wait_send()

        return 0

    lax.fori_loop(0, sweeps, drain, 0)

    @pl.when(row < rows_n - 1)
    def _():
        last_copy().wait_send()


def local(rows_n, cols_n, eigvecs, reflectors, factors, order, offsets):
    sweeps, _, span, width = reflectors.shape
    height, columns = eigvecs.shape
    part = (width, columns)
    vmem = pl.BlockSpec(memory_space=pltpu.VMEM)
    smem = pl.BlockSpec(memory_space=pltpu.SMEM)
    dma = pltpu.SemaphoreType.DMA
    return pl.pallas_call(
        functools.partial(kernel, rows_n, cols_n),
        out_shape=jax.ShapeDtypeStruct((height, columns), jnp.float32),
        in_specs=[smem, smem, vmem, vmem, vmem],
        out_specs=vmem,
        scratch_shapes=[
            pltpu.VMEM((cols_n, sweeps, span, span), jnp.float32),
            pltpu.VMEM((sweeps + 1, height + 2 * span, columns), jnp.float32),
            pltpu.VMEM((sweeps, 2) + part, jnp.float32),
            pltpu.VMEM((sweeps,) + part, jnp.float32),
            pltpu.VMEM((sweeps,) + part, jnp.float32),
            pltpu.VMEM(part, jnp.float32),
            dma((cols_n - 1, sweeps)),
            dma((cols_n, sweeps)),
            dma((sweeps, 2)),
            dma((sweeps, 2)),
            dma((sweeps,)),
            dma((sweeps,)),
            dma,
            dma,
        ],
        compiler_params=pltpu.CompilerParams(collective_id=0, has_side_effects=True),
    )(order, offsets, eigvecs, reflectors, factors)


def solution(mesh):
    placed = (
        P("row", "col"),
        P(None, ("row", "col"), None, None),
        P(None, ("row", "col"), None, None),
        P(),
        P(),
    )
    body = functools.partial(local, mesh.shape["row"], mesh.shape["col"])
    return jax.shard_map(
        body, mesh=mesh, in_specs=placed, out_specs=P("row", "col"), check_vma=False
    )
```

time: 721 us -> 95.6 us (0.13)
  blocking collectives: 592 us -> 0 us
  Pallas kernels: 0 us -> 91 us
  matrix products: 39.6 us -> 0 us
  local copies, waits for them, and re-layouts: 32.3 us -> 3.51 us
  loops' own time: 24.8 us -> 0 us
  between operations: 16.3 us -> 0.01 us
  starting transfers between devices: 11.5 us -> 0 us
    all_gather x32 -> x0, blocking collectives: 592 us -> none  [the longest x16 505 us: entering(): everything = jax.tree.map(lambda part: lax.all_gather(part, axis), array)]
    pallas_call x0 -> x1, Pallas kernels: none -> 91 us  [local(): pl.pallas_call(functools.partial(kernel, rows_n, cols_n), out_shape=jax.S...]
    dot_general x168 -> x0, matrix products: 39.6 us -> none  [the longest x64 13.4 us: compose(): jnp.dot(later[0], earlier[1], precision=highest, preferred_element_type=j...]
    dynamic_update_slice x32 -> x0, local copies, waits for them, and re-layouts: 28.9 us -> none  [advance(): lax.dynamic_update_slice_in_dim(current, reflect(segment, householder, tr...]
    another operation x16 -> x0, loops' own time: 24.8 us -> none  [the longest x8 22.6 us: sweep_apply(): return lax.fori_loop(0, house_set.shape[0], advance, extended)]
    ppermute x8 -> x0, starting transfers between devices: 11.5 us -> none  [passed_along(): return lax.ppermute(block, axis, route)]
  transfers between devices with their start and end apart: 8 -> 0, of which waited for: 0 -> 0; matrix products, arithmetic and copies ran while one was open for 0% -> 0% of each run, Pallas kernels for 0% -> 0%
where the time goes in v2:
time: 95.6 us; the launch traced here: 94.5 us
  Pallas kernels  91 us (95%)
  local copies, waits for them, and re-layouts  3.51 us (4%)
    pallas_call x1, Pallas kernels, local(): pl.pallas_call(functools.partial(kernel, rows_n, cols_n), out_shape=jax.S...  91 us
    unnamed x2, local copies, waits for them, and re-layouts  3.51 us

profile of v2, /device:TPU:30, one launch (start us, length us, event | category | flops | bytes accessed | tf_op | source)
XLA Modules:
  0.0 94.5 jit_solution(10987409455993707659)
XLA Ops:
  0.0 1.9 %copy.6.house_ref = f32[8,1,128,64]{3,2,1,0:T(8,128)} copy(f32[8,1,128,64]{2,3,1,0:T(8,128)} %param.6) | data formatting | bytes 524288 | tf_op args[1]
  1.9 91.0 %shard_map.55 = f32[256,128]{1,0:T(8,128)} custom-call(s32[8]{0:T(128)} %order_ref.1, s32[8]{0:T(128)} %off_ref.1, f32[256,128]{1,0:T(8,128)} %x_ref.1, f32[8,1,128,64]{3,2,1,0:T(8,128)} %copy.6.house_ref, f32[8,1,64,64]{3,2,1,0:T(8,128)} %tri_ref.1), custom_call_target="tpu_custom_call" | custom-call | tf_op jit(solution)/shard_map/pallas_call | solution.py:233
  92.9 1.6 %copy.8 = f32[256,128]{1,0:T(8,128)} copy(f32[256,128]{1,0:T(8,128)} %shard_map.55) | data formatting | bytes 262144

commit v3 on v2

v3 whole, which is shorter than its diff:
```python
import functools

import jax
import jax.numpy as jnp
from jax import lax
from jax.experimental import pallas as pl
from jax.experimental.pallas import tpu as pltpu
from jax.sharding import PartitionSpec as P

MESH = pl.DeviceIdType.MESH
highest = lax.Precision.HIGHEST


def split(x):
    hi = x.astype(jnp.bfloat16)
    lo = (x - hi.astype(jnp.float32)).astype(jnp.bfloat16)
    return hi, lo


def product(a, b):
    a_hi, a_lo = split(a)
    b_hi, b_lo = split(b)
    dot = functools.partial(jnp.dot, preferred_element_type=jnp.float32)
    return dot(a_hi, b_hi) + (dot(a_hi, b_lo) + dot(a_lo, b_hi))


def kernel(
    rows_n, cols_n, order_ref, off_ref, x_ref, house_ref, tri_ref, out_ref,
    maps, frames, up_in, down_in, down_out, last_in,
    map_send, map_recv, extra_send, extra_recv,
    up_send, up_recv, down_send, down_recv, last_send, last_recv,
):
    row, col = lax.axis_index("row"), lax.axis_index("col")
    sweeps, span = maps.shape[1], maps.shape[2]
    pairs = sweeps // 2
    width = span // 2
    height, columns = x_ref.shape
    per = height // width
    pad = span
    first = row == 0
    above, below = row > 0, row < rows_n - 1
    odd = lax.rem(col, 2)
    near = col + 1 - 2 * odd
    far = lax.rem(col + cols_n // 2, cols_n)
    low = col < 2

    def send(src, dst, sent, got, to_row, to_col):
        return pltpu.make_async_remote_copy(
            src_ref=src, dst_ref=dst, send_sem=sent, recv_sem=got,
            device_id=(to_row, to_col), device_id_type=MESH,
        )

    def map_copy(kind, p):
        slot = far if kind == 2 else col
        place = maps.at[slot, p]
        to = far if kind == 1 else near
        return send(place, place, map_send.at[kind, p], map_recv.at[slot, p], row, to)

    def map_arrival(j, p):
        return send(maps.at[j, p], maps.at[j, p], map_send.at[0, p], map_recv.at[j, p], row, near)

    def extra_up(t):
        return send(
            maps.at[col, 2 * t], maps.at[cols_n + odd, 2 * t],
            extra_send.at[0, t], extra_recv.at[odd, t], row - 1, col,
        )

    def extra_copy(kind, t, slot):
        place = maps.at[cols_n + slot, 2 * t]
        to = far if kind == 2 else near
        return send(place, place, extra_send.at[kind, t], extra_recv.at[slot, t], row, to)

    def up_copy(t, part, src):
        return send(
            src, up_in.at[t, part], up_send.at[t, part], up_recv.at[t, part], row - 1, col
        )

    def down_copy(q):
        return send(
            down_out.at[q], down_in.at[q], down_send.at[q], down_recv.at[q], row + 1, col
        )

    def last_copy():
        return send(
            frames.at[sweeps, pl.ds(pad + height - width, width)], last_in,
            last_send, last_recv, row + 1, col,
        )

    barrier = pltpu.get_barrier_semaphore()

    def greet(to_row, to_col):
        pl.semaphore_signal(
            barrier, inc=1, device_id=(to_row, to_col), device_id_type=MESH
        )

    greet(row, near)
    greet(row, far)

    @pl.when(above)
    def _():
        greet(row - 1, col)

    @pl.when(below)
    def _():
        greet(row + 1, col)

    def dense(p):
        house = house_ref[order_ref[p], 0]
        tri = tri_ref[order_ref[p], 0]
        scaled = jnp.dot(house, tri, precision=highest, preferred_element_type=jnp.float32)
        inner = lax.dot_general(
            scaled, house, (((1,), (1,)), ((), ())), precision=highest,
            preferred_element_type=jnp.float32,
        )
        eye = lax.broadcasted_iota(jnp.int32, inner.shape, 0) == lax.broadcasted_iota(
            jnp.int32, inner.shape, 1
        )
        maps[col, p] = jnp.where(eye, 1.0, 0.0) - inner

    dense(0)
    frames[0, pl.ds(pad, height), :] = x_ref[...]
    greeted = 2 + jnp.minimum(row, 1) + jnp.minimum(rows_n - 1 - row, 1)
    pl.semaphore_wait(barrier, greeted)
    map_copy(1, 0).start()
    map_copy(0, 0).start()

    @pl.when(above)
    def _():
        for part in range(per):
            up_copy(0, part, x_ref.at[pl.ds(part * width, width)]).start()

    @pl.when(above & low)
    def _():
        extra_up(0).start()

    def spread(p, _):
        dense(p)
        map_copy(1, p).start()
        map_copy(0, p).start()

        @pl.when(above & low & (lax.rem(p, 2) == 0))
        def _():
            extra_up(p // 2).start()

        return 0

    def relay(t):
        for q in (2 * t, 2 * t + 1):
            map_arrival(far, q).wait_recv()
            map_copy(2, q).start()

        @pl.when(below)
        def _():
            extra_copy(1, t, odd).wait_recv()
            extra_copy(1, t, odd).start()

            @pl.when(low)
            def _():
                extra_copy(2, t, odd).start()

    lax.fori_loop(1, sweeps, spread, 0)
    relay(0)

    blank = jnp.zeros((width, columns), jnp.float32)

    def pair(t, _):
        a, b = 2 * t, 2 * t + 1
        start_a, start_b = off_ref[order_ref[a]], off_ref[order_ref[b]]
        before = jnp.where(t == 0, 0, off_ref[order_ref[jnp.maximum(a - 1, 0)]])
        shift = {0: start_a - before, 1: start_b - start_a}
        start = {0: start_a, 1: start_b}
        for q in (a, b):
            for j in range(cols_n):

                @pl.when((col != j) & (far != j))
                def _(j=j, q=q):
                    map_arrival(j, q).wait_recv()

        @pl.when(below)
        def _():
            extra_copy(1, t, 1 - odd).wait_recv()

        def fresh(n, j):
            rows = frames[a + n, pl.ds(pad + (j + 1) * width + shift[n], width), :]
            index = row * height + (j + 1) * width + start[n]
            index = index + lax.broadcasted_iota(jnp.int32, rows.shape, 0)
            return jnp.where(index < rows_n * height, rows, 0.0)

        def early(n, j):
            return product(maps[j, a + n], jnp.concatenate([blank, fresh(n, j)], 0))

        def late(n, j, ready, carried):
            return ready + product(maps[j, a + n], jnp.concatenate([carried, blank], 0))

        def put(n, j, value):
            frames[a + n + 1, pl.ds(pad + j * width, width), :] = value

        def arrive(part):
            @pl.when(below)
            def _():
                up_copy(t, part, up_in.at[t, part]).wait_recv()

            frames[a, pl.ds(pad + height + part * width, width), :] = up_in[t, part]

        def lead(n):
            put(n, -1, frames[a + n, pl.ds(pad - width + shift[n], width), :])
            return frames[a + n, pl.ds(pad + shift[n], width), :]

        def entry(n, own):
            @pl.when(above)
            def _():
                down_copy(a + n).wait_recv()

            return jnp.where(first, own, down_in[a + n])

        def leave(n, carried):
            down_out[a + n] = carried

            @pl.when(below)
            def _():
                down_copy(a + n).start()

        def lift(part):
            @pl.when(above & (t < pairs - 1))
            def _():
                place = frames.at[a + 2, pl.ds(pad + part * width, width)]
                up_copy(t + 1, part, place).start()

        ready = [early(0, j) for j in range(per - 2)]
        carried = entry(0, lead(0))
        for j in range(per):
            if j >= per - 2:
                arrive(j - (per - 2))
                ready.append(early(0, j))
            both = late(0, j, ready[j], carried)
            put(0, j, both[:width])
            carried = both[width:]
        leave(0, carried)

        @pl.when(t < pairs - 1)
        def _():
            relay(t + 1)

        ready = [early(1, j) for j in range(per - 2)]
        own = lead(1)
        arrive(2)
        next_ready = early(0, per)
        other = entry(1, own)
        low_out = late(1, 0, ready[0], other)
        high_out = late(0, per, next_ready, carried)
        put(0, per, high_out[:width])
        put(1, 0, low_out[:width])
        lift(0)
        arrive(3)
        next_ready = early(0, per + 1)
        high_out = late(0, per + 1, next_ready, high_out[width:])
        put(0, per + 1, high_out[:width])
        other = low_out[width:]
        for j in range(1, per):
            if j >= per - 2:
                ready.append(early(1, j))
            both = late(1, j, ready[j], other)
            put(1, j, both[:width])
            other = both[width:]
            if j < per - 1:
                lift(j)
        leave(1, other)
        lift(per - 1)
        return 0

    lax.fori_loop(0, pairs, pair, 0)

    @pl.when(below)
    def _():
        last_copy().start()

    @pl.when(above)
    def _():
        last_copy().wait_recv()

    edge = frames[sweeps, pl.ds(pad - width, width), :]
    frames[sweeps, pl.ds(pad - width, width), :] = jnp.where(first, edge, last_in[...])
    shift_back = off_ref[order_ref[sweeps - 1]]
    out_ref[...] = frames[sweeps, pl.ds(pad - shift_back, height), :]

    def drain(t, _):
        for q in (2 * t, 2 * t + 1):
            for kind in range(3):
                map_copy(kind, q).wait_send()

            @pl.when(below)
            def _(q=q):
                down_copy(q).wait_send()

        @pl.when(above)
        def _():
            for part in range(per):
                up_copy(t, part, up_in.at[t, part]).wait_send()

            @pl.when(low)
            def _():
                extra_up(t).wait_send()

        @pl.when(below)
        def _():
            extra_copy(1, t, odd).wait_send()

            @pl.when(low)
            def _():
                extra_copy(2, t, odd).wait_send()

        return 0

    lax.fori_loop(0, pairs, drain, 0)

    @pl.when(below)
    def _():
        last_copy().wait_send()


def local(rows_n, cols_n, eigvecs, reflectors, factors, order, offsets):
    sweeps, _, span, width = reflectors.shape
    height, columns = eigvecs.shape
    part = (width, columns)
    vmem = pl.BlockSpec(memory_space=pltpu.VMEM)
    smem = pl.BlockSpec(memory_space=pltpu.SMEM)
    dma = pltpu.SemaphoreType.DMA
    return pl.pallas_call(
        functools.partial(kernel, rows_n, cols_n),
        out_shape=jax.ShapeDtypeStruct((height, columns), jnp.float32),
        in_specs=[smem, smem, vmem, vmem, vmem],
        out_specs=vmem,
        scratch_shapes=[
            pltpu.VMEM((cols_n + 2, sweeps, span, span), jnp.float32),
            pltpu.VMEM((sweeps + 1, 2 * height + span, columns), jnp.float32),
            pltpu.VMEM((sweeps // 2, height // width) + part, jnp.float32),
            pltpu.VMEM((sweeps,) + part, jnp.float32),
            pltpu.VMEM((sweeps,) + part, jnp.float32),
            pltpu.VMEM(part, jnp.float32),
            dma((3, sweeps)),
            dma((cols_n, sweeps)),
            dma((3, sweeps // 2)),
            dma((2, sweeps // 2)),
            dma((sweeps // 2, height // width)),
            dma((sweeps // 2, height // width)),
            dma((sweeps,)),
            dma((sweeps,)),
            dma,
            dma,
        ],
        compiler_params=pltpu.CompilerParams(collective_id=0, has_side_effects=True),
    )(order, offsets, eigvecs, reflectors, factors)


def solution(mesh):
    placed = (
        P("row", "col"),
        P(None, ("row", "col"), None, None),
        P(None, ("row", "col"), None, None),
        P(),
        P(),
    )
    body = functools.partial(local, mesh.shape["row"], mesh.shape["col"])
    return jax.shard_map(
        body, mesh=mesh, in_specs=placed, out_specs=P("row", "col"), check_vma=False
    )
```

time: 95.6 us -> 80.7 us (0.84)
  Pallas kernels: 91 us -> 77 us
    pallas_call x1, Pallas kernels: 91 us -> 77 us  [local(): pl.pallas_call(functools.partial(kernel, rows_n, cols_n), out_shape=jax.S...]
where the time goes in v3:
time: 80.7 us; the launch traced here: 80.5 us
  Pallas kernels  77 us (95%)
  local copies, waits for them, and re-layouts  3.51 us (4%)
    pallas_call x1, Pallas kernels, local(): pl.pallas_call(functools.partial(kernel, rows_n, cols_n), out_shape=jax.S...  77 us
    unnamed x2, local copies, waits for them, and re-layouts  3.51 us

profile of v3, /device:TPU:30, one launch (start us, length us, event | category | flops | bytes accessed | tf_op | source)
XLA Modules:
  0.0 80.5 jit_solution(2755258812118714742)
XLA Ops:
  0.0 1.9 %copy.6.house_ref = f32[8,1,128,64]{3,2,1,0:T(8,128)} copy(f32[8,1,128,64]{2,3,1,0:T(8,128)} %param.6) | data formatting | bytes 524288 | tf_op args[1]
  1.9 77.0 %shard_map.55 = f32[256,128]{1,0:T(8,128)} custom-call(s32[8]{0:T(128)} %order_ref.1, s32[8]{0:T(128)} %off_ref.1, f32[256,128]{1,0:T(8,128)} %x_ref.1, f32[8,1,128,64]{3,2,1,0:T(8,128)} %copy.6.house_ref, f32[8,1,64,64]{3,2,1,0:T(8,128)} %tri_ref.1), custom_call_target="tpu_custom_call" | custom-call | tf_op jit(solution)/shard_map/pallas_call | solution.py:328
  78.9 1.6 %copy.8 = f32[256,128]{1,0:T(8,128)} copy(f32[256,128]{1,0:T(8,128)} %shard_map.55) | data formatting | bytes 262144

commit v4 on v3

--- a/solution.py
+++ b/solution.py
@@ -26,7 +26,7 @@
 
 def kernel(
     rows_n, cols_n, order_ref, off_ref, x_ref, house_ref, tri_ref, out_ref,
-    maps, frames, up_in, down_in, down_out, last_in,
+    maps, frames, up_in, down_in, down_out, last_in, response,
     map_send, map_recv, extra_send, extra_recv,
     up_send, up_recv, down_send, down_recv, last_send, last_recv,
 ):
@@ -107,9 +107,9 @@
     def dense(p):
         house = house_ref[order_ref[p], 0]
         tri = tri_ref[order_ref[p], 0]
-        scaled = jnp.dot(house, tri, precision=highest, preferred_element_type=jnp.float32)
+        scaled = jnp.dot(tri, house, precision=highest, preferred_element_type=jnp.float32)
         inner = lax.dot_general(
-            scaled, house, (((1,), (1,)), ((), ())), precision=highest,
+            house, scaled, (((0,), (0,)), ((), ())), precision=highest,
             preferred_element_type=jnp.float32,
         )
         eye = lax.broadcasted_iota(jnp.int32, inner.shape, 0) == lax.broadcasted_iota(
@@ -226,46 +226,59 @@
                 place = frames.at[a + 2, pl.ds(pad + part * width, width)]
                 up_copy(t + 1, part, place).start()
 
-        ready = [early(0, j) for j in range(per - 2)]
-        carried = entry(0, lead(0))
+        def respond(n):
+            block = maps[0, a + n][:, :width]
+            for j in range(per):
+                if j:
+                    block = product(maps[j, a + n][:, :width], block[width:])
+                response[n, pl.ds(j * width, width), :] = block[:width]
+            response[n, pl.ds(per * width, width), :] = block[width:]
+
+        def idle(n, j, carried):
+            ready = early(n, j)
+            if carried is not None:
+                ready = late(n, j, ready, carried)
+            return ready
+
+        def settle(n, parts, own):
+            whole = jnp.concatenate(parts, 0) + product(response[n], entry(n, own))
+            for j in range(per):
+                put(n, j, whole[j * width : (j + 1) * width])
+            carried = whole[per * width :]
+            leave(n, carried)
+            return carried
+
+        respond(0)
+        respond(1)
+        parts, carried = [], None
+        own = lead(0)
         for j in range(per):
             if j >= per - 2:
                 arrive(j - (per - 2))
-                ready.append(early(0, j))
-            both = late(0, j, ready[j], carried)
-            put(0, j, both[:width])
+            both = idle(0, j, carried)
+            parts.append(both[:width])
             carried = both[width:]
-        leave(0, carried)
+        carried = settle(0, parts + [carried], own)
 
         @pl.when(t < pairs - 1)
         def _():
             relay(t + 1)
 
-        ready = [early(1, j) for j in range(per - 2)]
         own = lead(1)
         arrive(2)
-        next_ready = early(0, per)
-        other = entry(1, own)
-        low_out = late(1, 0, ready[0], other)
-        high_out = late(0, per, next_ready, carried)
-        put(0, per, high_out[:width])
-        put(1, 0, low_out[:width])
-        lift(0)
         arrive(3)
-        next_ready = early(0, per + 1)
-        high_out = late(0, per + 1, next_ready, high_out[width:])
-        put(0, per + 1, high_out[:width])
-        other = low_out[width:]
-        for j in range(1, per):
-            if j >= per - 2:
-                ready.append(early(1, j))
-            both = late(1, j, ready[j], other)
-            put(1, j, both[:width])
+        parts, other = [], None
+        for j in range(per):
+            if j < 2:
+                both = late(0, per + j, early(0, per + j), carried)
+                put(0, per + j, both[:width])
+                carried = both[width:]
+            both = idle(1, j, other)
+            parts.append(both[:width])
             other = both[width:]
-            if j < per - 1:
-                lift(j)
-        leave(1, other)
-        lift(per - 1)
+        settle(1, parts + [other], own)
+        for j in range(per):
+            lift(j)
         return 0
 
     lax.fori_loop(0, pairs, pair, 0)
@@ -337,6 +350,7 @@
             pltpu.VMEM((sweeps,) + part, jnp.float32),
             pltpu.VMEM((sweeps,) + part, jnp.float32),
             pltpu.VMEM(part, jnp.float32),
+            pltpu.VMEM((2, height + width, width), jnp.float32),
             dma((3, sweeps)),
             dma((cols_n, sweeps)),
             dma((3, sweeps // 2)),
@@ -349,7 +363,7 @@
             dma,
         ],
         compiler_params=pltpu.CompilerParams(collective_id=0, has_side_effects=True),
-    )(order, offsets, eigvecs, reflectors, factors)
+    )(order, offsets, eigvecs, jnp.swapaxes(reflectors, 2, 3), factors)
 
 
 def solution(mesh):

time: 80.7 us -> 76 us (0.942)
  Pallas kernels: 77 us -> 74.2 us
  local copies, waits for them, and re-layouts: 3.51 us -> 1.57 us
    pallas_call x1, Pallas kernels: 77 us -> 74.2 us  [local(): pl.pallas_call(functools.partial(kernel, rows_n, cols_n), out_shape=jax.S...]
    unnamed x2 -> x1, local copies, waits for them, and re-layouts: 3.51 us -> 1.57 us
where the time goes in v4:
time: 76 us; the launch traced here: 75.8 us
  Pallas kernels  74.2 us (98%)
  local copies, waits for them, and re-layouts  1.57 us (2%)
    pallas_call x1, Pallas kernels, local(): pl.pallas_call(functools.partial(kernel, rows_n, cols_n), out_shape=jax.S...  74.2 us
    unnamed x1, local copies, waits for them, and re-layouts  1.57 us

profile of v4, /device:TPU:30, one launch (start us, length us, event | category | flops | bytes accessed | tf_op | source)
XLA Modules:
  0.0 75.8 jit_solution(1711045792607231400)
XLA Ops:
  0.0 74.2 %shard_map.55 = f32[256,128]{1,0:T(8,128)} custom-call(s32[8]{0:T(128)} %order_ref.1, s32[8]{0:T(128)} %off_ref.1, f32[256,128]{1,0:T(8,128)} %x_ref.1, f32[8,1,64,128]{3,2,1,0:T(8,128)} %bitcast.1, f32[8,1,64,64]{3,2,1,0:T(8,128)} %tri_ref.1), custom_call_target="tpu_custom_call" | custom-call | tf_op jit(solution)/shard_map/pallas_call | solution.py:341
  74.2 1.6 %copy.7 = f32[256,128]{1,0:T(8,128)} copy(f32[256,128]{1,0:T(8,128)} %shard_map.55) | data formatting | bytes 262144

commit v5 on v4

--- a/solution.py
+++ b/solution.py
@@ -133,17 +133,6 @@
     def _():
         extra_up(0).start()
 
-    def spread(p, _):
-        dense(p)
-        map_copy(1, p).start()
-        map_copy(0, p).start()
-
-        @pl.when(above & low & (lax.rem(p, 2) == 0))
-        def _():
-            extra_up(p // 2).start()
-
-        return 0
-
     def relay(t):
         for q in (2 * t, 2 * t + 1):
             map_arrival(far, q).wait_recv()
@@ -158,7 +147,17 @@
             def _():
                 extra_copy(2, t, odd).start()
 
-    lax.fori_loop(1, sweeps, spread, 0)
+    for p in range(1, sweeps):
+        dense(p)
+    for p in range(1, sweeps):
+        map_copy(1, p).start()
+        map_copy(0, p).start()
+
+    @pl.when(above & low)
+    def _():
+        for t in range(1, pairs):
+            extra_up(t).start()
+
     relay(0)
 
     blank = jnp.zeros((width, columns), jnp.float32)

time: 76 us -> 76.3 us (level)
  no operation moved by 1% of the time
where the time goes in v5:
time: 76.3 us; the launch traced here: 76.1 us
  Pallas kernels  74.6 us (98%)
  local copies, waits for them, and re-layouts  1.57 us (2%)
    pallas_call x1, Pallas kernels, local(): pl.pallas_call(functools.partial(kernel, rows_n, cols_n), out_shape=jax.S...  74.6 us
    unnamed x1, local copies, waits for them, and re-layouts  1.57 us

profile of v5, /device:TPU:30, one launch (start us, length us, event | category | flops | bytes accessed | tf_op | source)
XLA Modules:
  0.0 76.1 jit_solution(9257004434305554864)
XLA Ops:
  0.0 74.6 %shard_map.55 = f32[256,128]{1,0:T(8,128)} custom-call(s32[8]{0:T(128)} %order_ref.1, s32[8]{0:T(128)} %off_ref.1, f32[256,128]{1,0:T(8,128)} %x_ref.1, f32[8,1,64,128]{3,2,1,0:T(8,128)} %bitcast.1, f32[8,1,64,64]{3,2,1,0:T(8,128)} %tri_ref.1), custom_call_target="tpu_custom_call" | custom-call | tf_op jit(solution)/shard_map/pallas_call | solution.py:340
  74.6 1.6 %copy.7 = f32[256,128]{1,0:T(8,128)} copy(f32[256,128]{1,0:T(8,128)} %shard_map.55) | data formatting | bytes 262144
